TPU v7x, 32 devices: a whole 2x2x4 slice. The times are simulated.
32 devices in a mesh: dp: 2 (over x), seq: 16 (over z, y, core).
Axes of the slice: x: 2, y: 2, z: 4, core: 2. Of those that a mesh axis runs over, the one named last changes fastest.
Arguments:
- tiles: bfloat16 [2, 16, 32, 4, 1024], P('dp', None, 'seq'), may hold values from -6 to 6
- patch_index: int32 [2, 16, 32, 4], P('dp', None, 'seq'), may hold values from 0 to 127
- pos_table: bfloat16 [128, 1024], replicated, may hold values from -6 to 6
- depth_kernel: bfloat16 [2, 27, 1024], replicated, may hold values from -1.25 to 1.25
- enc_gain: bfloat16 [2, 1024], replicated, may hold values from 0.099609375 to 1.8984375
- point_weight: bfloat16 [2, 1024, 1024], replicated, may hold values from -0.1875 to 0.1875
- action_ids: int32 [2, 16], replicated, may hold values from 0 to 7
- w_in: bfloat16 [1024, 5120], P('seq', 'dp'), may hold values from -0.1875 to 0.1875
- action_table: bfloat16 [8, 5120], P(None, 'dp'), may hold values from -6 to 6
- dyn_gain: bfloat16 [5120], P('dp'), may hold values from 0.099609375 to 1.8984375
- w_query: bfloat16 [5120, 5120], P('seq', 'dp'), may hold values from -0.078125 to 0.078125
- w_keyval: bfloat16 [5120, 2, 1024], P('seq', None, 'dp'), may hold values from -0.078125 to 0.078125
- seq_order: int32 [4], replicated, may hold values from 0 to 3, each once
Outputs:
- attended: bfloat16 [2, 16, 32, 4, 5120], P(None, None, 'seq', None, 'dp')
Inputs may be any that keep to these rules, and one draw needn't show every extreme that they name: `seq_order`: each of 0 to 3 appears once.
All inputs are finite; a program needn't handle non-finite values.
Results may differ from a plain program's by a relative error of at most 0.012.
Values may be sent and summed in bfloat16 or wider, within the bound.
A program may use at most 128 MiB of HBM per device.

v0:
```python
import jax
import jax.numpy as jnp
from jax import lax
from jax.sharding import PartitionSpec as P

DIM = 5120
HEAD = 128
Q_HEADS = 40
KV_HEADS = 8


def extended(block, sides, width):
    for axis, dim in sides:
        count = lax.axis_size(axis)
        forward = [(i, i + 1) for i in range(count - 1)]
        backward = [(target, source) for source, target in forward]
        low = lax.ppermute(
            lax.slice_in_dim(block, block.shape[dim] - width, None, axis=dim), axis, forward
        )
        high = lax.ppermute(lax.slice_in_dim(block, 0, width, axis=dim), axis, backward)
        block = jnp.concatenate([low, block, high], axis=dim)
    return block


def depth_block(padded, kernel, gains, weight):
    frames = padded.shape[1]
    height = padded.shape[2] - 2
    breadth = padded.shape[3]
    channels = padded.shape[4]
    framed = jnp.pad(padded.astype(jnp.float32), ((0, 0), (2, 0), (0, 0), (1, 1), (0, 0)))
    summed = jnp.zeros((padded.shape[0], frames, height, breadth, channels), jnp.float32)
    for time_tap in range(3):
        for row_tap in range(3):
            for col_tap in range(3):
                window = framed[
                    :,
                    time_tap : time_tap + frames,
                    row_tap : row_tap + height,
                    col_tap : col_tap + breadth,
                    :,
                ]
                summed = summed + window * kernel[9 * time_tap + 3 * row_tap + col_tap].astype(
                    jnp.float32
                )
    factor = lax.rsqrt(jnp.mean(summed * summed, axis=-1, keepdims=True) + 1e-05)
    normed = (summed * factor * gains.astype(jnp.float32)).astype(jnp.bfloat16)
    projected = jnp.dot(
        normed.reshape(-1, channels), weight, preferred_element_type=jnp.float32
    ).reshape(summed.shape)
    centre = padded[:, :, 1:-1].astype(jnp.float32)
    return (centre + jax.nn.gelu(projected)).astype(jnp.bfloat16)


def body(
    tiles,
    patch_index,
    pos_table,
    depth_kernel,
    enc_gain,
    point_weight,
    action_ids,
    w_in,
    action_table,
    dyn_gain,
    w_query,
    w_keyval,
    seq_order,
):
    frames = tiles.shape[1]
    height = tiles.shape[2]
    breadth = tiles.shape[3]
    channels = tiles.shape[4]
    positions = pos_table.shape[0]
    blocks = depth_kernel.shape[0]
    flat_index = patch_index.reshape(-1)
    position_pick = (flat_index[:, None] == jnp.arange(positions, dtype=jnp.int32)[None, :]).astype(
        jnp.bfloat16
    )
    placed = jnp.dot(position_pick, pos_table, preferred_element_type=jnp.float32).reshape(
        tiles.shape
    )
    hidden = (tiles.astype(jnp.float32) + placed).astype(jnp.bfloat16)
    for block_idx in range(blocks):
        padded = extended(hidden, (("seq", 2),), 1)
        hidden = depth_block(
            padded, depth_kernel[block_idx], enc_gain[block_idx], point_weight[block_idx]
        )
    latent = hidden.reshape(-1, channels)
    clips = action_ids.shape[0]
    actions = action_table.shape[0]
    cells = height * breadth
    action_range = jnp.arange(actions, dtype=jnp.int32)
    gathered = lax.all_gather(latent, "dp", axis=0, tiled=True)
    w_slab = lax.all_gather(w_in, "seq", axis=0, tiled=True)
    action_pick = (action_ids.reshape(-1)[:, None] == action_range[None, :]).astype(jnp.bfloat16)
    action_rows = jnp.dot(action_pick, action_table, preferred_element_type=jnp.float32)
    embed = jnp.dot(gathered, w_slab, preferred_element_type=jnp.float32).reshape(
        clips * frames, cells, -1
    )
    embed = jax.nn.gelu(embed + action_rows[:, None, :])
    squares = lax.psum(jnp.sum(embed * embed, axis=-1), "dp")
    factor = lax.rsqrt(squares / DIM + 1e-05)[:, :, None]
    normed = (
        (embed * factor * dyn_gain.astype(jnp.float32))
        .astype(jnp.bfloat16)
        .reshape(clips * frames * cells, -1)
    )
    inputs = lax.all_gather(normed, "dp", axis=1, tiled=True)
    pieces = (
        lax.all_gather(w_query, "seq", axis=0, tiled=True),
        lax.all_gather(w_keyval, "seq", axis=0, tiled=True),
    )
    span_rows = pieces[0].shape[0]
    query_sum = jnp.dot(inputs, pieces[0], preferred_element_type=jnp.float32)
    pair_sum = jnp.dot(inputs, pieces[1].reshape(span_rows, -1), preferred_element_type=jnp.float32)
    kv_local = w_keyval.shape[2] // HEAD
    group = Q_HEADS // KV_HEADS
    query_heads = query_sum.reshape(clips, frames, cells, kv_local, group, HEAD)
    pairs = pair_sum.reshape(clips, frames, cells, 2, kv_local, HEAD)
    key_heads = pairs[:, :, :, 0]
    value_heads = pairs[:, :, :, 1].astype(jnp.bfloat16)
    query_unit = query_heads * lax.rsqrt(
        jnp.mean(query_heads * query_heads, axis=-1, keepdims=True) + 1e-06
    )
    key_unit = key_heads * lax.rsqrt(
        jnp.mean(key_heads * key_heads, axis=-1, keepdims=True) + 1e-06
    )
    scores = jnp.einsum(
        "cfpkgh,ctpkh->cpkgft", query_unit, key_unit, precision=lax.Precision.HIGHEST
    ) * HEAD ** (-0.5)
    causal = (
        jnp.arange(frames, dtype=jnp.int32)[:, None] >= jnp.arange(frames, dtype=jnp.int32)[None, :]
    )
    raised = jnp.where(causal, jnp.exp(scores), 0.0)
    shares = (raised / jnp.sum(raised, axis=-1, keepdims=True)).astype(jnp.bfloat16)
    mixed = jnp.einsum(
        "cpkgft,ctpkh->cfpkgh", shares, value_heads, preferred_element_type=jnp.float32
    ).astype(jnp.bfloat16)
    mixed = mixed.reshape(clips, frames, height, breadth, -1)
    return jnp.take(mixed, seq_order, axis=3)


def solution(mesh):
    placed = (
        P("dp", None, "seq", None, None),
        P("dp", None, "seq", None),
        P(),
        P(),
        P(),
        P(),
        P(),
        P("seq", "dp"),
        P(None, "dp"),
        P("dp"),
        P("seq", "dp"),
        P("seq", None, "dp"),
        P(),
    )
    return jax.shard_map(
        body,
        mesh=mesh,
        in_specs=placed,
        out_specs=P(None, None, "seq", None, "dp"),
        check_vma=False,
    )
```

profile of v0, /device:TPU:7, one launch (start us, length us, event | category | flops | bytes accessed | tf_op | source)
XLA Modules:
  0.0 373.9 jit_solution(16638443497301449434)
XLA Ops:
  6.6 0.7 all-gather.5.cloned.1.call-update
  7.3 0.7 all-gather.9.cloned.1.call-update
  8.1 0.8 copy.46
  9.7 2.6 collective-permute-start.1
  12.3 3.9 %collective-permute-start = (bf16[1,16,1,4,1024]{4,3,2,1,0:T(4,128)(2,1)S(1)}, bf16[1,16,1,4,1024]{4,3,2,1,0:T(4,128)(2,1)S(1)}, u32[]{:S(2)}, u32[]{:S(2)}) collective-permute-start(bf16[1,16,1,4,1024]{4,3,2,1,0:T(4,128)(2,1)S(1)} %get-tuple-element.11), channel_id=1, source_target_pairs={{0,1},{1,2},{2,3},{3,4},{4,5},{5,6},{6,7},{7,8},{8,9},{9,10},{10,1... | collective-permute-start | bytes 393224 | tf_op jit(solution)/shard_map/ppermute | solution.py:17
  16.4 1.0 fusion.141
  17.4 0.7 collective-permute-done
  18.4 4.4 %multiply_reduce_fusion.4 = (f32[16,2,4]{2,1,0:T(2,128)S(1)}, f32[1,16,2,4,1024]{4,3,2,1,0:T(4,128)S(1)}) fusion(f32[1024]{0:T(1024)S(1)} %bitcast.139, f32[1024]{0:T(1024)S(1)} %bitcast.140, f32[1,16,4,4,1024]{4,3,2,1,0:T(4,128)S(1)} %maximum_convert_fusion, f32[1024]{0:T(1024)S(1)} %bitcast.141, f32[1024]{0:T(1024)S(1)} %bitcast.142, ...), kind=kLoop, calls=%fused_computation.212 | loop fusion | flops 7208832 | bytes 3256832 | tf_op jit(solution)/shard_map/reduce_sum | solution.py:45
  23.4 2.1 fusion.12
  26.1 2.8 collective-permute-start.3
  28.9 4.4 %collective-permute-start.2 = (bf16[1,16,1,4,1024]{4,3,2,1,0:T(4,128)(2,1)S(1)}, bf16[1,16,1,4,1024]{4,3,2,1,0:T(4,128)(2,1)S(1)}, u32[]{:S(2)}, u32[]{:S(2)}) collective-permute-start(bf16[1,16,1,4,1024]{4,3,2,1,0:T(4,128)(2,1)S(1)} %get-tuple-element.9), channel_id=1, source_target_pairs={{0,1},{1,2},{2,3},{3,4},{4,5},{5,6},{6,7},{7,8},{8,9},{9,10},{10,1... | collective-permute-start | bytes 393224 | tf_op jit(solution)/shard_map/ppermute | solution.py:17
  33.4 1.4 collective-permute-done.3
  35.6 4.4 %multiply_reduce_fusion.3 = (f32[16,2,4]{2,1,0:T(2,128)S(1)}, f32[1,16,2,4,1024]{4,3,2,1,0:T(4,128)S(1)}) fusion(f32[1024]{0:T(1024)S(1)} %bitcast.117, f32[1024]{0:T(1024)S(1)} %bitcast.118, f32[1,16,4,4,1024]{4,3,2,1,0:T(4,128)S(1)} %maximum_convert_fusion.1, f32[1024]{0:T(1024)S(1)} %bitcast.153, f32[1024]{0:T(1024)S(1)} %bitcast.154, ...), kind=kLoop, calls=%fused_computation.210 | loop fusion | flops 7208832 | bytes 3256832 | tf_op jit(solution)/shard_map/reduce_sum | solution.py:45
  40.5 2.1 fusion.10
  43.2 7.5 %all_gather.15 = bf16[256,1024]{1,0:T(8,128)(2,1)S(1)} all-gather(bf16[128,1024]{1,0:T(8,128)(2,1)S(1)} %reshape.924), channel_id=1, replica_groups=mesh['dp'=2,'seq'=16] {'dp'}, dimensions={0}, use_global_device_ids=true | all-gather | bytes 786432 | tf_op jit(solution)/shard_map/all_gather | solution.py:93
  50.7 15.4 %all-gather.5.cloned.1.call-done = bf16[1024,2560]{1,0:T(8,128)(2,1)} async-done(((bf16[64,2560]{1,0:T(8,128)(2,1)}), bf16[1024,2560]{1,0:T(8,128)(2,1)}) %all-gather.5.cloned.1.call-update) | async-done | bytes 5242896 | tf_op jit(solution)/shard_map/all_gather | solution.py:94
  66.1 4.6 %multiply_reduce_fusion.1 = (f32[256]{0:T(256)S(1)}, f32[256,2560]{1,0:T(8,128)S(1)}) fusion(f32[32,2560]{1,0:T(8,128)} %fusion.141, bf16[256,1024]{1,0:T(8,128)(2,1)S(1)} %all_gather.15, bf16[1024,2560]{1,0:T(8,128)(2,1)} %all-gather.5.cloned.1.call-done), kind=kOutput, calls=%fused_computation.64 | convolution fusion | flops 1349385984 | bytes 8717312 | tf_op jit(solution)/shard_map/dot_general | solution.py:97
  70.8 5.2 %psum.7 = f32[32,8]{1,0:T(8,128)S(1)} all-reduce(f32[32,8]{1,0:T(8,128)S(1)} %reduce_sum.59), channel_id=1, replica_groups=mesh['dp'=2,'seq'=16] {'dp'}, use_global_device_ids=true, to_apply=%region_3.4 | all-reduce | flops 256 | bytes 2048 | tf_op jit(solution)/shard_map/psum | solution.py:101
  76.1 1.3 multiply_convert_fusion
  78.1 76.4 %all-gather.9.cloned.1.call-done = bf16[5120,2,512]{2,1,0:T(2,128)(2,1)} async-done(((bf16[320,2,512]{2,1,0:T(2,128)(2,1)}), bf16[5120,2,512]{2,1,0:T(2,128)(2,1)}) %all-gather.9.cloned.1.call-update) | async-done | bytes 10485776 | tf_op jit(solution)/shard_map/all_gather | solution.py:111
  154.5 26.3 %copy.63 = bf16[5120,2,512]{0,2,1:T(8,128)(2,1)} copy(bf16[5120,2,512]{2,1,0:T(2,128)(2,1)} %all-gather.9.cloned.1.call-done) | data formatting | bytes 20971520 | tf_op jit(solution)/shard_map/reshape | solution.py:115
  180.9 11.9 %all-gather.7.cloned.1.call-done = bf16[256,5120]{1,0:T(8,128)(2,1)} async-done(((bf16[256,2560]{1,0:T(8,128)(2,1)}), bf16[256,5120]{1,0:T(8,128)(2,1)}) %all-gather.7.cloned.1.call-update) | async-done | bytes 2621456 | tf_op jit(solution)/shard_map/all_gather | solution.py:108
  192.8 6.5 %fusion.149 = f32[2,16,8,2,4,128]{5,2,4,3,1,0:T(8,128)S(1)} fusion(bf16[2,16,8,5120,1,1]{3,2,5,4,1,0:T(8,128)(2,1)} %bitcast.173, bf16[2,4,128,5120,1,1]{3,2,1,0,5,4:T(8,128)(2,1)} %bitcast.114), kind=kOutput, calls=%fused_computation.292 | convolution fusion | flops 2684354560 | bytes 14155776 | tf_op jit(solution)/shard_map/dot_general | solution.py:115
  199.8 129.1 %all-gather.11.cloned.1.call-done = bf16[5120,2560]{1,0:T(8,128)(2,1)} async-done(((bf16[320,2560]{1,0:T(8,128)(2,1)}), bf16[5120,2560]{1,0:T(8,128)(2,1)}) %all-gather.11.cloned.1.call-update) | async-done | bytes 26214416 | tf_op jit(solution)/shard_map/all_gather | solution.py:110
  329.0 12.8 %fusion.150 = f32[256,2560]{1,0:T(8,128)S(1)} fusion(bf16[256,5120]{1,0:T(8,128)(2,1)} %all-gather.7.cloned.1.call-done, bf16[5120,2560]{1,0:T(8,128)(2,1)} %all-gather.11.cloned.1.call-done), kind=kOutput, calls=%fused_computation.293 | convolution fusion | flops 6710886400 | bytes 31457280 | tf_op jit(solution)/shard_map/dot_general | solution.py:114
  341.7 0.7 multiply_reduce_fusion
  342.6 0.8 broadcast_multiply_fusion
  343.4 15.7 %fusion.9 = (f32[2,8,4,5,16]{4,3,2,1,0:T(8,128)S(1)}, f32[2,8,4,16,16,5]{4,3,5,2,1,0:T(8,128)S(1)}) fusion(pred[16,16]{0,1:T(8,128)(4,1)S(1)} %iota_compare_fusion.4, f32[2,16,8,4,5,128]{5,2,4,3,1,0:T(8,128)S(1)} %broadcast_multiply_fusion, f32[2,16,8,4,128,1]{4,2,3,1,0,5:T(8,128)S(1)} %multiply_bitcast_fusion), kind=kOutput, calls=%fused_computation.65 | convolution fusion | flops 126069760 | bytes 3494144 | tf_op jit(solution)/shard_map/cfpkgh,ctpkh->cpkgft/dot_general | solution.py:128
  359.1 1.2 fusion.16
  360.8 2.3 reshape.927
  363.1 2.0 gather_fusion
  365.3 2.1 copy.57
  (69 shorter events, 6.7 us)
Async XLA Ops:
  6.5 2.5 copy-start
  6.5 2.9 copy-start.3
  6.5 9.6 %copy-start.7 = (s32[2,16]{1,0:T(2,128)S(1)}, s32[2,16]{1,0:T(2,128)}, u32[]{:S(2)}) copy-start(s32[2,16]{1,0:T(2,128)} %param.19) | copy-start | bytes 388
  6.5 9.7 %copy-start.6 = (bf16[2560]{0:T(1024)(128)(2,1)S(1)}, bf16[2560]{0:T(1024)(128)(2,1)}, u32[]{:S(2)}) copy-start(bf16[2560]{0:T(1024)(128)(2,1)} %param.22) | copy-start | bytes 15364
  6.5 9.7 %copy-start.2 = (bf16[2,27,1024]{2,0,1:T(2,128)(2,1)S(1)}, bf16[2,27,1024]{2,0,1:T(2,128)(2,1)}, u32[]{:S(2)}) copy-start(bf16[2,27,1024]{2,0,1:T(2,128)(2,1)} %param.16) | copy-start | bytes 331780
  6.5 9.9 %copy-start.4 = (bf16[8,2560]{1,0:T(8,128)(2,1)S(1)}, bf16[8,2560]{1,0:T(8,128)(2,1)}, u32[]{:S(2)}) copy-start(bf16[8,2560]{1,0:T(8,128)(2,1)} %param.21) | copy-start | bytes 122884
  6.6 10.8 %copy-start.5 = (bf16[2,1024]{1,0:T(2,128)(2,1)S(1)}, bf16[2,1024]{1,0:T(2,128)(2,1)}, u32[]{:S(2)}) copy-start(bf16[2,1024]{1,0:T(2,128)(2,1)} %param.17) | copy-start | bytes 12292
  6.6 59.5 %all-gather.5.cloned.1.call-start = ((), (), s32[]{:S(2)}) async-start(), calls=%async_computation | async-start | bytes 5570560 | tf_op jit(solution)/shard_map/all_gather | solution.py:94
  7.3 147.2 %all-gather.9.cloned.1.call-start = ((), (), s32[]{:S(2)}) async-start(), calls=%async_computation.2 | async-start | bytes 11141120 | tf_op jit(solution)/shard_map/all_gather | solution.py:111
  8.1 184.7 %all-gather.7.cloned.1.call-start = ((), (), s32[]{:S(2)}) async-start(), calls=%async_computation.1 | async-start | bytes 3932160 | tf_op jit(solution)/shard_map/all_gather | solution.py:108
  9.7 7.7 %collective-permute-start.1 = (bf16[1,16,1,4,1024]{4,3,2,1,0:T(4,128)(2,1)S(1)}, bf16[1,16,1,4,1024]{4,3,2,1,0:T(4,128)(2,1)S(1)}, u32[]{:S(2)}, u32[]{:S(2)}) collective-permute-start(bf16[1,16,1,4,1024]{4,3,2,1,0:T(4,128)(2,1)S(1)} %get-tuple-element.12), channel_id=1, source_target_pairs={{1,0},{2,1},{3,2},{4,3},{5,4},{6,5},{7,6},{8,7},{9,8},{10,9},{11,1... | collective-permute-start | bytes 393224 | tf_op jit(solution)/shard_map/ppermute | solution.py:20
  12.3 5.8 %collective-permute-start = (bf16[1,16,1,4,1024]{4,3,2,1,0:T(4,128)(2,1)S(1)}, bf16[1,16,1,4,1024]{4,3,2,1,0:T(4,128)(2,1)S(1)}, u32[]{:S(2)}, u32[]{:S(2)}) collective-permute-start(bf16[1,16,1,4,1024]{4,3,2,1,0:T(4,128)(2,1)S(1)} %get-tuple-element.11), channel_id=1, source_target_pairs={{0,1},{1,2},{2,3},{3,4},{4,5},{5,6},{6,7},{7,8},{8,9},{9,10},{10,1... | collective-permute-start | bytes 393224 | tf_op jit(solution)/shard_map/ppermute | solution.py:17
  26.1 8.6 %collective-permute-start.3 = (bf16[1,16,1,4,1024]{4,3,2,1,0:T(4,128)(2,1)S(1)}, bf16[1,16,1,4,1024]{4,3,2,1,0:T(4,128)(2,1)S(1)}, u32[]{:S(2)}, u32[]{:S(2)}) collective-permute-start(bf16[1,16,1,4,1024]{4,3,2,1,0:T(4,128)(2,1)S(1)} %get-tuple-element.10), channel_id=1, source_target_pairs={{1,0},{2,1},{3,2},{4,3},{5,4},{6,5},{7,6},{8,7},{9,8},{10,9},{11,1... | collective-permute-start | bytes 393224 | tf_op jit(solution)/shard_map/ppermute | solution.py:20
  28.9 6.3 %collective-permute-start.2 = (bf16[1,16,1,4,1024]{4,3,2,1,0:T(4,128)(2,1)S(1)}, bf16[1,16,1,4,1024]{4,3,2,1,0:T(4,128)(2,1)S(1)}, u32[]{:S(2)}, u32[]{:S(2)}) collective-permute-start(bf16[1,16,1,4,1024]{4,3,2,1,0:T(4,128)(2,1)S(1)} %get-tuple-element.9), channel_id=1, source_target_pairs={{0,1},{1,2},{2,3},{3,4},{4,5},{5,6},{6,7},{7,8},{8,9},{9,10},{10,1... | collective-permute-start | bytes 393224 | tf_op jit(solution)/shard_map/ppermute | solution.py:17
  76.1 2.0 copy-start.8
  77.5 251.5 %all-gather.11.cloned.1.call-start = ((), (), s32[]{:S(2)}) async-start(), calls=%async_computation.3 | async-start | bytes 27852800 | tf_op jit(solution)/shard_map/all_gather | solution.py:110
  363.1 4.3 %copy-start.1 = (bf16[128,1024]{1,0:T(8,128)(2,1)S(1)}, bf16[128,1024]{1,0:T(8,128)(2,1)}, u32[]{:S(2)}) copy-start(bf16[128,1024]{1,0:T(8,128)(2,1)} %param.15) | copy-start | bytes 786436
Sparse Core Ops, SparseCore 0:
  9.7 56.3 all-gather.4
  68.4 86.0 all-gather.8
  156.1 36.6 all-gather.6
  194.2 134.6 all-gather.10
where the time goes:
time: 376 us; the launch traced here: 374 us
  waiting for transfers between devices  237 us (63%)
  matrix products  46.1 us (12%)
  local copies, waits for them, and re-layouts  35.7 us (9%)
  other arithmetic  14.9 us (4%)
  starting transfers between devices  14 us (4%)
  between operations  13.5 us (4%)
  blocking collectives  12.7 us (3%)
    all_gather x1, waiting for transfers between devices, body(): lax.all_gather(w_query, 'seq', axis=0, tiled=True)  129 us
    all_gather x1, waiting for transfers between devices, body(): lax.all_gather(w_keyval, 'seq', axis=0, tiled=True)  76.4 us
    reshape x1, local copies, waits for them, and re-layouts, body(): pieces[1].reshape(span_rows, -1)  26.3 us
    dot_general x1, matrix products, body(): jnp.einsum('cfpkgh,ctpkh->cpkgft', query_unit, key_unit, precision=lax.Pr...  15.7 us
    all_gather x1, waiting for transfers between devices, body(): w_slab = lax.all_gather(w_in, 'seq', axis=0, tiled=True)  15.4 us
    dot_general x1, matrix products, body(): query_sum = jnp.dot(inputs, pieces[0], preferred_element_type=jnp.float32)  12.8 us
    all_gather x1, waiting for transfers between devices, body(): inputs = lax.all_gather(normed, 'dp', axis=1, tiled=True)  11.9 us
    reduce_sum x2, other arithmetic, depth_block(): jnp.mean(summed * summed, axis=-1, keepdims=True) + 1e-05  8.87 us
  transfers between devices with their start and end apart: 8, of which 7 were waited for; matrix products, arithmetic and copies ran while one was open for 16% of the time, Pallas kernels for 0%

commit v1 on v0

v1 whole, which is shorter than its diff:
```python
import functools
import math

import jax
import jax.numpy as jnp
from jax import lax
from jax.experimental import pallas as pl
from jax.experimental.pallas import tpu as pltpu
from jax.sharding import PartitionSpec as P

DIM = 5120
HEAD = 128
Q_HEADS = 40
KV_HEADS = 8
MESH = pl.DeviceIdType.MESH


def extended(block, sides, width):
    for axis, dim in sides:
        count = lax.axis_size(axis)
        forward = [(i, i + 1) for i in range(count - 1)]
        backward = [(target, source) for source, target in forward]
        low = lax.ppermute(
            lax.slice_in_dim(block, block.shape[dim] - width, None, axis=dim), axis, forward
        )
        high = lax.ppermute(lax.slice_in_dim(block, 0, width, axis=dim), axis, backward)
        block = jnp.concatenate([low, block, high], axis=dim)
    return block


def depth_block(padded, kernel, gains, weight):
    frames = padded.shape[1]
    height = padded.shape[2] - 2
    breadth = padded.shape[3]
    channels = padded.shape[4]
    framed = jnp.pad(padded.astype(jnp.float32), ((0, 0), (2, 0), (0, 0), (1, 1), (0, 0)))
    summed = jnp.zeros((padded.shape[0], frames, height, breadth, channels), jnp.float32)
    for time_tap in range(3):
        for row_tap in range(3):
            for col_tap in range(3):
                window = framed[
                    :,
                    time_tap : time_tap + frames,
                    row_tap : row_tap + height,
                    col_tap : col_tap + breadth,
                    :,
                ]
                summed = summed + window * kernel[9 * time_tap + 3 * row_tap + col_tap].astype(
                    jnp.float32
                )
    factor = lax.rsqrt(jnp.mean(summed * summed, axis=-1, keepdims=True) + 1e-05)
    normed = (summed * factor * gains.astype(jnp.float32)).astype(jnp.bfloat16)
    projected = jnp.dot(
        normed.reshape(-1, channels), weight, preferred_element_type=jnp.float32
    ).reshape(summed.shape)
    centre = padded[:, :, 1:-1].astype(jnp.float32)
    return (centre + jax.nn.gelu(projected)).astype(jnp.bfloat16)


def gelu(z):
    return 0.5 * z * (1.0 + jnp.tanh(0.7978845608028654 * (z + 0.044715 * (z * z * z))))


def flipped(t, mask, bits):
    for bit in bits:
        if mask & bit:
            t = t + bit - 2 * bit * ((t // bit) % 2)
    return t


def window_kernel(
    sizes,
    pack_ref,
    in_ref,
    aux_ref,
    latent_ref,
    pick_ref,
    out_ref,
    w_all,
    in_all,
    aux_all,
    lat_all,
    embeds,
    squares,
    mixed,
    w_send,
    w_recv,
    i_send,
    i_recv,
    l_send,
    l_recv,
    a_send,
    a_recv,
    o_send,
    o_recv,
    own_sem,
):
    D, C, T, cells, kvg = sizes
    d = lax.axis_index("dp")
    seq = lax.axis_index("seq")
    c = seq // T
    t = seq % T
    bits = []
    bit = T // 2
    while bit:
        bits.append(bit)
        bit //= 2
    depth = pack_ref.shape[1]
    in_rows, in_cols = in_ref.shape
    tokens = latent_ref.shape[0]
    group = Q_HEADS // KV_HEADS
    qcols = kvg * group * HEAD

    def to_c(shift):
        return (d, ((c + shift) % C) * T + t)

    def to_t(bit):
        return (d, c * T + flipped(t, bit, bits))

    def to_d(shift):
        return ((d + shift) % D, seq)

    peers = [to_c(s) for s in range(1, C)] + [to_t(b) for b in bits] + [to_d(s) for s in range(1, D)]
    barrier = pltpu.get_barrier_semaphore()
    for peer in peers:
        pl.semaphore_signal(barrier, inc=1, device_id=peer, device_id_type=MESH)
    pl.semaphore_wait(barrier, len(peers))

    sends = []

    def push(src, dst, send_sem, recv_sem, peer):
        copy = pltpu.make_async_remote_copy(
            src_ref=src,
            dst_ref=dst,
            send_sem=send_sem,
            recv_sem=recv_sem,
            device_id=peer,
            device_id_type=MESH,
        )
        copy.start()
        sends.append(copy)

    def arrived(ref, sem):
        pltpu.make_async_copy(ref, ref, sem).wait()

    def w_slot(s, m):
        origin = ((c + C - s) % C) * T + flipped(t, m, bits)
        return w_all.at[pl.ds(pl.multiple_of(origin * depth, depth), depth)]

    def i_slot(s, m, e):
        origin = ((c + C - s) % C) * T + flipped(t, m, bits)
        column = ((d + D - e) % D) * in_cols
        return in_all.at[
            pl.ds(pl.multiple_of(origin * in_rows, in_rows), in_rows),
            pl.ds(pl.multiple_of(column, HEAD), in_cols),
        ]

    def l_slot(s, e):
        row = ((d + D - e) % D) * tokens
        return lat_all.at[(c + C - s) % C, pl.ds(pl.multiple_of(row, tokens), tokens)]

    def a_slot(e):
        column = ((d + D - e) % D) * in_cols
        return aux_all.at[:, pl.ds(pl.multiple_of(column, HEAD), in_cols)]

    def w_forward(s, m, src):
        low = -1
        for b in bits:
            if m & b:
                low = bits.index(b)
        for index in range(low + 1, len(bits)):
            b = bits[index]
            push(src, w_slot(s, m), w_send.at[s, m | b], w_recv.at[s, m | b], to_t(b))

    early, last = bits[:-1], bits[-1]

    def i_forward(s, m, e, src):
        low = -1
        for b in early:
            if m & b:
                low = bits.index(b)
        if e == 0:
            for index in range(low + 1, len(early)):
                b = early[index]
                push(src, i_slot(s, m, e), i_send.at[s, m | b, e], i_recv.at[s, m | b, e], to_t(b))
            for shift in range(1, D):
                push(src, i_slot(s, m, e), i_send.at[s, m, shift], i_recv.at[s, m, shift], to_d(shift))
        push(src, i_slot(s, m, e), i_send.at[s, m | last, e], i_recv.at[s, m | last, e], to_t(last))

    def l_forward(s, src):
        for e in range(1, D):
            push(src, l_slot(s, 0), l_send.at[s, e], l_recv.at[s, e], to_d(e))

    own = [
        pltpu.make_async_copy(pack_ref.at[c], w_slot(0, 0), own_sem.at[0]),
        pltpu.make_async_copy(in_ref, i_slot(0, 0, 0), own_sem.at[1]),
        pltpu.make_async_copy(latent_ref, l_slot(0, 0), own_sem.at[2]),
        pltpu.make_async_copy(aux_ref, a_slot(0), own_sem.at[3]),
    ]
    for copy in own:
        copy.start()
    for shift in range(1, D):
        push(aux_ref, a_slot(0), a_send.at[shift], a_recv.at[shift], to_d(shift))
    for shift in range(1, C):
        push(in_ref, i_slot(0, 0, 0), i_send.at[shift, 0, 0], i_recv.at[shift, 0, 0], to_c(shift))
    i_forward(0, 0, 0, in_ref)
    for shift in range(1, C):
        push(latent_ref, l_slot(0, 0), l_send.at[shift, 0], l_recv.at[shift, 0], to_c(shift))
    l_forward(0, latent_ref)
    for shift in range(1, C):
        push(
            pack_ref.at[(c + shift) % C],
            w_slot(0, 0),
            w_send.at[shift, 0],
            w_recv.at[shift, 0],
            to_c(shift),
        )
    w_forward(0, 0, pack_ref.at[c])

    def i_event(s, m, e):
        arrived(i_slot(s, m, e), i_recv.at[s, m, e])
        if not m & last:
            i_forward(s, m, e, i_slot(s, m, e))

    def w_event(s, m):
        arrived(w_slot(s, m), w_recv.at[s, m])
        w_forward(s, m, w_slot(s, m))

    def l_event(s, e):
        arrived(l_slot(s, e), l_recv.at[s, e])
        if e == 0:
            l_forward(s, l_slot(s, e))

    order_w = sorted(
        ((m.bit_count(), s, m) for s in range(C) for m in range(T) if s or m),
        key=lambda item: (item[0] + item[1], item[0]),
    )
    w_todo = [(s, m) for _, s, m in order_w]
    for s in range(1, C):
        i_event(s, 0, 0)
    for m in sorted((m for m in range(1, T) if not m & last), key=lambda m: m.bit_count()):
        for s in range(C):
            i_event(s, m, 0)
    for s in range(1, C):
        l_event(s, 0)
    for e in range(1, D):
        arrived(a_slot(e), a_recv.at[e])
        for m in range(T):
            if not m & last:
                for s in range(C):
                    i_event(s, m, e)
    for s, m in list(w_todo):
        if m == 0:
            w_event(s, m)
            w_todo.remove((s, m))
    for m in range(T):
        if m & last:
            for e in range(D):
                for s in range(C):
                    i_event(s, m, e)
    for e in range(1, D):
        for s in range(C):
            l_event(s, e)
    for copy in own:
        copy.wait()

    chunk = 512
    rows = D * tokens

    def embed_block(shift):
        where = (c + shift) % C
        squares[where] = jnp.zeros((rows, HEAD), jnp.float32)

        def step(j, carry):
            cols = pl.ds(pl.multiple_of(j * chunk, chunk), chunk)
            z = jnp.dot(lat_all[where], in_all[:, cols], preferred_element_type=jnp.float32)
            z = z + jnp.dot(pick_ref[...], aux_all[:, cols], preferred_element_type=jnp.float32)
            g = gelu(z)
            gain = aux_all[:, cols].astype(jnp.float32)[8:9]
            embeds[where, :, cols] = (g * gain).astype(jnp.bfloat16)
            square = g * g
            part = square[:, :HEAD]
            for k in range(1, chunk // HEAD):
                part = part + square[:, k * HEAD : (k + 1) * HEAD]
            squares[where] += part
            return carry

        lax.fori_loop(0, embeds.shape[2] // chunk, step, 0)

    per = -(-len(w_todo) // C)
    for shift in range(C):
        embed_block(shift)
        for s, m in w_todo[shift * per : (shift + 1) * per]:
            w_event(s, m)

    row_ids = lax.broadcasted_iota(jnp.int32, (tokens, tokens), 0)
    col_ids = lax.broadcasted_iota(jnp.int32, (tokens, tokens), 1)
    seen = (row_ids % cells == col_ids % cells) & (row_ids // cells >= col_ids // cells)

    def unit(x):
        return x * lax.rsqrt(jnp.mean(x * x, axis=-1, keepdims=True) + 1e-06)

    def mix_block(where):
        total = jnp.dot(embeds[where], w_all[...], preferred_element_type=jnp.float32)
        mean = jnp.sum(squares[where], axis=-1, keepdims=True) / DIM
        total = total * lax.rsqrt(mean + 1e-05)
        for kv in range(kvg):
            at = qcols + kv * HEAD
            key = unit(total[:, at : at + HEAD]).astype(jnp.bfloat16)
            at = qcols + (kvg + kv) * HEAD
            value = total[:, at : at + HEAD].astype(jnp.bfloat16)
            for h in range(kv * group, (kv + 1) * group):
                query = unit(total[:, h * HEAD : (h + 1) * HEAD]) * HEAD**-0.5
                query = query.astype(jnp.bfloat16)
                for clip in range(D):
                    span = slice(clip * tokens, (clip + 1) * tokens)
                    score = lax.dot_general(
                        query[span],
                        key[span],
                        (((1,), (1,)), ((), ())),
                        preferred_element_type=jnp.float32,
                    )
                    raised = jnp.where(seen, jnp.exp(score), 0.0)
                    shares = raised / jnp.sum(raised, axis=-1, keepdims=True)
                    result = jnp.dot(
                        shares.astype(jnp.bfloat16), value[span], preferred_element_type=jnp.float32
                    )
                    mixed[where, span, h * HEAD : (h + 1) * HEAD] = result.astype(jnp.bfloat16)

    mine = pl.ds(pl.multiple_of(c * qcols, HEAD), qcols)

    def send_of(shift):
        where = (c + shift) % C
        return pltpu.make_async_remote_copy(
            src_ref=mixed.at[where],
            dst_ref=out_ref.at[:, mine],
            send_sem=o_send.at[shift],
            recv_sem=o_recv.at[shift],
            device_id=(d, where * T + t),
            device_id_type=MESH,
        )

    def mix_step(index, carry):
        shift = index + 1
        mix_block((c + shift) % C)
        send_of(shift).start()
        return carry

    lax.fori_loop(0, C - 1, mix_step, 0)
    mix_block(c)
    keep = pltpu.make_async_copy(mixed.at[c], out_ref.at[:, mine], own_sem.at[0])
    keep.start()
    for shift in range(1, C):
        send_of(shift).wait_send()
        column = ((c + C - shift) % C) * qcols
        arrived(out_ref.at[:, pl.ds(pl.multiple_of(column, HEAD), qcols)], o_recv.at[shift])
    keep.wait()
    for copy in sends:
        copy.wait_send()


def body(
    tiles,
    patch_index,
    pos_table,
    depth_kernel,
    enc_gain,
    point_weight,
    action_ids,
    w_in,
    action_table,
    dyn_gain,
    w_query,
    w_keyval,
    seq_order,
):
    clip_local, frames, height, breadth, channels = tiles.shape
    positions = pos_table.shape[0]
    blocks = depth_kernel.shape[0]
    D, S = lax.axis_size("dp"), lax.axis_size("seq")
    kv_local = w_keyval.shape[2] // HEAD
    C = math.gcd(kv_local, S)
    T = S // C
    assert T & (T - 1) == 0 and T > 1 and clip_local == 1
    kvg = kv_local // C
    group = Q_HEADS // KV_HEADS
    depth = w_query.shape[0]

    flat_index = patch_index.reshape(-1)
    position_pick = (flat_index[:, None] == jnp.arange(positions, dtype=jnp.int32)[None, :]).astype(
        jnp.bfloat16
    )
    placed = jnp.dot(position_pick, pos_table, preferred_element_type=jnp.float32).reshape(
        tiles.shape
    )
    hidden = (tiles.astype(jnp.float32) + placed).astype(jnp.bfloat16)
    for block_idx in range(blocks):
        padded = extended(hidden, (("seq", 2),), 1)
        hidden = depth_block(
            padded, depth_kernel[block_idx], enc_gain[block_idx], point_weight[block_idx]
        )
    latent = jnp.take(hidden, seq_order, axis=3).reshape(-1, channels)

    cells = height * breadth
    tokens = frames * cells
    pack = jnp.concatenate(
        [
            w_query.reshape(depth, C, -1).transpose(1, 0, 2),
            w_keyval.reshape(depth, 2, C, -1).transpose(2, 0, 1, 3).reshape(C, depth, -1),
        ],
        axis=2,
    )
    actions = action_table.shape[0]
    assert actions == 8
    aux = jnp.concatenate(
        [action_table, dyn_gain[None], jnp.zeros((7, action_table.shape[1]), jnp.bfloat16)], axis=0
    )
    pick = (
        jnp.repeat(action_ids.reshape(-1), cells)[:, None] == jnp.arange(16, dtype=jnp.int32)[None]
    ).astype(jnp.bfloat16)
    width = pack.shape[2]
    qcols = kvg * group * HEAD
    bf16, f32 = jnp.bfloat16, jnp.float32
    dma = pltpu.SemaphoreType.DMA
    out = pl.pallas_call(
        functools.partial(window_kernel, (D, C, T, cells, kvg)),
        out_shape=jax.ShapeDtypeStruct((D * tokens, C * qcols), bf16),
        in_specs=[pl.BlockSpec(memory_space=pltpu.VMEM)] * 5,
        out_specs=pl.BlockSpec(memory_space=pltpu.VMEM),
        scratch_shapes=[
            pltpu.VMEM((S * depth, width), bf16),
            pltpu.VMEM((channels, DIM), bf16),
            pltpu.VMEM((16, DIM), bf16),
            pltpu.VMEM((C, D * tokens, channels), bf16),
            pltpu.VMEM((C, D * tokens, DIM), bf16),
            pltpu.VMEM((C, D * tokens, HEAD), f32),
            pltpu.VMEM((C, D * tokens, qcols), bf16),
            dma((C, T)),
            dma((C, T)),
            dma((C, T, D)),
            dma((C, T, D)),
            dma((C, D)),
            dma((C, D)),
            dma((D,)),
            dma((D,)),
            dma((C,)),
            dma((C,)),
            dma((4,)),
        ],
        compiler_params=pltpu.CompilerParams(
            collective_id=0, has_side_effects=True, vmem_limit_bytes=60 * 1024 * 1024
        ),
    )(pack, w_in, aux, latent, pick)
    return out.reshape(D, frames, height, breadth, -1)


def solution(mesh):
    placed = (
        P("dp", None, "seq", None, None),
        P("dp", None, "seq", None),
        P(),
        P(),
        P(),
        P(),
        P(),
        P("seq", "dp"),
        P(None, "dp"),
        P("dp"),
        P("seq", "dp"),
        P("seq", None, "dp"),
        P(),
    )
    return jax.shard_map(
        body,
        mesh=mesh,
        in_specs=placed,
        out_specs=P(None, None, "seq", None, "dp"),
        check_vma=False,
    )
```

time: 376 us -> 232 us (0.62)
  waiting for transfers between devices: 237 us -> 0.01 us
  Pallas kernels: 0 us -> 176 us
  matrix products: 46.1 us -> 6.17 us
  local copies, waits for them, and re-layouts: 35.7 us -> 14.9 us
  between operations: 13.5 us -> 0.59 us
  blocking collectives: 12.7 us -> 0 us
  other arithmetic: 14.9 us -> 19.8 us
    all_gather x4 -> x0, waiting for transfers between devices: 233 us -> none  [the longest x1 129 us: body(): lax.all_gather(w_query, 'seq', axis=0, tiled=True)]
    pallas_call x0 -> x1, Pallas kernels: none -> 176 us  [body(): pl.pallas_call(functools.partial(window_kernel, (D, C, T, cells, kvg)), o...]
    dot_general x6 -> x0, matrix products: 41.7 us -> none  [the longest x1 15.7 us: body(): jnp.einsum('cfpkgh,ctpkh->cpkgft', query_unit, key_unit, precision=lax.Pr...]
    reshape x3 -> x4, local copies, waits for them, and re-layouts: 28.7 us -> 6.09 us  [the longest x1 3.5 us: body(): return out.reshape(D, frames, height, breadth, -1)]
    all_gather x1 -> x0, blocking collectives: 7.47 us -> none  [body(): gathered = lax.all_gather(latent, 'dp', axis=0, tiled=True)]
    psum x1 -> x0, blocking collectives: 5.19 us -> none  [body(): squares = lax.psum(jnp.sum(embed * embed, axis=-1), 'dp')]
  transfers between devices with their start and end apart: 8 -> 4, of which waited for: 7 -> 0; matrix products, arithmetic and copies ran while one was open for 16% -> 6% of each run, Pallas kernels for 0% -> 0%
where the time goes in v1:
time: 232 us; the launch traced here: 231 us
  Pallas kernels  176 us (76%)
  other arithmetic  19.8 us (9%)
  local copies, waits for them, and re-layouts  14.9 us (6%)
  starting transfers between devices  13.1 us (6%)
  matrix products  6.17 us (3%)
    pallas_call x1, Pallas kernels, body(): pl.pallas_call(functools.partial(window_kernel, (D, C, T, cells, kvg)), o...  176 us
    ppermute x2, starting transfers between devices, extended(): lax.ppermute(lax.slice_in_dim(block, block.shape[dim] - width, None, axis...  8.6 us
    reduce_sum x2, other arithmetic, depth_block(): jnp.mean(summed * summed, axis=-1, keepdims=True) + 1e-05  6.62 us
    dot_general x2, matrix products, depth_block(): jnp.dot(normed.reshape(-1, channels), weight, preferred_element_type=jnp....  4.96 us
  transfers between devices with their start and end apart: 4, of which 0 were waited for; matrix products, arithmetic and copies ran while one was open for 6% of the time, Pallas kernels for 0%

profile of v1, /device:TPU:7, one launch (start us, length us, event | category | flops | bytes accessed | tf_op | source)
XLA Modules:
  0.0 231.0 jit_solution(9293883975369558093)
XLA Ops:
  0.0 0.8 copy.35
  1.0 1.2 fusion.127
  2.3 1.4 fusion.124
  3.7 0.7 fusion.132
  4.4 2.6 %collective-permute-start.1 = (bf16[1,16,1,4,1024]{4,1,3,2,0:T(8,128)(2,1)}, bf16[1,16,1,4,1024]{4,1,3,2,0:T(8,128)(2,1)S(1)}, u32[]{:S(2)}, u32[]{:S(2)}) collective-permute-start(bf16[1,16,1,4,1024]{4,1,3,2,0:T(8,128)(2,1)} %get-tuple-element.12), channel_id=1, source_target_pairs={{1,0},{2,1},{3,2},{4,3},{5,4},{6,5},{7,6},{8,7},{9,8},{10,9},{11,1... | collective-permute-start | bytes 393224 | tf_op jit(solution)/shard_map/ppermute | solution.py:26
  7.0 3.9 %collective-permute-start = (bf16[1,16,1,4,1024]{4,1,3,2,0:T(8,128)(2,1)}, bf16[1,16,1,4,1024]{4,1,3,2,0:T(8,128)(2,1)S(1)}, u32[]{:S(2)}, u32[]{:S(2)}) collective-permute-start(bf16[1,16,1,4,1024]{4,1,3,2,0:T(8,128)(2,1)} %get-tuple-element.11), channel_id=1, source_target_pairs={{0,1},{1,2},{2,3},{3,4},{4,5},{5,6},{6,7},{7,8},{8,9},{9,10},{10,1... | collective-permute-start | bytes 393224 | tf_op jit(solution)/shard_map/ppermute | solution.py:23
  10.9 0.7 slice_convert_fusion.55
  11.6 0.7 slice_convert_fusion.26
  12.3 0.7 slice_convert_fusion.27
  13.9 1.6 copy.62
  15.5 0.6 slice_convert_fusion
  16.7 0.6 reshape.904
  17.3 0.7 broadcast_in_dim.26
  17.9 0.7 eq.34
  18.6 1.4 fusion.126.pick_ref
  20.1 0.7 maximum_maximum_fusion.aux_ref
  20.8 1.2 compare_and_fusion
  22.1 3.4 %multiply_reduce_fusion.1 = (f32[16,2,4]{0,2,1:T(4,128)S(1)}, f32[1,16,2,4,1024]{4,1,3,2,0:T(8,128)S(1)}) fusion(f32[1024]{0:T(1024)} %bitcast.126, f32[1024]{0:T(1024)} %bitcast.127, f32[1,16,4,4,1024]{4,1,3,2,0:T(8,128)S(1)} %maximum_convert_fusion, f32[1024]{0:T(1024)} %bitcast.128, f32[1024]{0:T(1024)} %bitcast.129, f32[1024]{0:T(1024)} %bitcast.130, ...), kind=kLoop, calls=%fused_computation.191 | loop fusion | flops 7208832 | bytes 3256832 | tf_op jit(solution)/shard_map/reduce_sum | solution.py:51
  25.9 0.8 reshape.900
  26.7 2.9 %fusion.2 = f32[128,1024]{1,0:T(8,128)} fusion(bf16[128,1024]{1,0:T(8,128)(2,1)} %reshape.900, bf16[2,1024,1024]{2,1,0:T(8,128)(2,1)} %param.18), kind=kOutput, calls=%fused_computation.52 | convolution fusion | flops 268435456 | bytes 2883584 | tf_op jit(solution)/shard_map/dot_general | solution.py:53
  29.6 2.0 reshape.901
  31.6 1.4 fusion.14
  33.0 0.7 fusion.131
  33.7 1.9 collective-permute-start.3
  35.6 4.7 %collective-permute-start.2 = (bf16[1,16,1,4,1024]{4,1,3,2,0:T(8,128)(2,1)}, bf16[1,16,1,4,1024]{4,1,3,2,0:T(8,128)(2,1)S(1)}, u32[]{:S(2)}, u32[]{:S(2)}) collective-permute-start(bf16[1,16,1,4,1024]{4,1,3,2,0:T(8,128)(2,1)} %get-tuple-element.9), channel_id=1, source_target_pairs={{0,1},{1,2},{2,3},{3,4},{4,5},{5,6},{6,7},{7,8},{8,9},{9,10},{10,1... | collective-permute-start | bytes 393224 | tf_op jit(solution)/shard_map/ppermute | solution.py:23
  40.5 1.6 pad_maximum_fusion.pack_ref
  42.3 0.6 pad_clamp_fusion
  43.2 3.2 %multiply_reduce_fusion = (f32[16,2,4]{0,2,1:T(4,128)S(1)}, f32[1,16,2,4,1024]{4,1,3,2,0:T(8,128)S(1)}) fusion(f32[1024]{0:T(1024)S(1)} %bitcast.85, f32[1024]{0:T(1024)S(1)} %bitcast.86, f32[1,16,4,4,1024]{4,1,3,2,0:T(8,128)S(1)} %maximum_convert_fusion.1, f32[1024]{0:T(1024)S(1)} %bitcast.94, f32[1024]{0:T(1024)S(1)} %bitcast.95, f32[1024]{0:T(1024)S(1)} %bitcast.96, ...), kind=kLoop, calls=%fused_computation.189 | loop fusion | flops 7208832 | bytes 3256832 | tf_op jit(solution)/shard_map/reduce_sum | solution.py:51
  46.8 2.0 fusion
  50.3 0.8 broadcast_select_fusion.latent_ref
  51.1 176.4 %shard_map.127 = bf16[256,2560]{1,0:T(8,128)(2,1)} custom-call(bf16[4,320,896]{2,1,0:T(8,128)(2,1)} %pad_maximum_fusion.pack_ref, bf16[64,2560]{1,0:T(8,128)(2,1)} %in_ref.1, bf16[16,2560]{1,0:T(8,128)(2,1)} %maximum_maximum_fusion.aux_ref, bf16[128,1024]{1,0:T(8,128)(2,1)} %broadcast_select_fusion.latent_ref, bf16[256,16]{1,0:T(8,128)(2,1)} %fusion.126.pick_ref), custom_call_target="tpu_custom_call" | custom-call | tf_op jit(solution)/shard_map/pallas_call | solution.py:425
  227.6 3.5 %reshape.905 = bf16[2,16,2,4,2560]{4,3,2,1,0:T(4,128)(2,1)} reshape(bf16[256,2560]{1,0:T(8,128)(2,1)} %shard_map.127) | data formatting | bytes 2621440 | tf_op jit(solution)/shard_map/reshape | solution.py:454
  (82 shorter events, 4.3 us)
Async XLA Ops:
  0.0 13.0 %copy-start = (bf16[320,2,512]{2,1,0:T(2,128)(2,1)S(1)}, bf16[320,2,512]{2,1,0:T(2,128)(2,1)}, u32[]{:S(2)}) copy-start(bf16[320,2,512]{2,1,0:T(2,128)(2,1)} %param.24) | copy-start | bytes 1966084
  0.0 10.9 %copy-start.1 = (bf16[2,27,1024]{2,0,1:T(2,128)(2,1)S(1)}, bf16[2,27,1024]{2,0,1:T(2,128)(2,1)}, u32[]{:S(2)}) copy-start(bf16[2,27,1024]{2,0,1:T(2,128)(2,1)} %param.16) | copy-start | bytes 331780
  4.4 17.6 %collective-permute-start.1 = (bf16[1,16,1,4,1024]{4,1,3,2,0:T(8,128)(2,1)}, bf16[1,16,1,4,1024]{4,1,3,2,0:T(8,128)(2,1)S(1)}, u32[]{:S(2)}, u32[]{:S(2)}) collective-permute-start(bf16[1,16,1,4,1024]{4,1,3,2,0:T(8,128)(2,1)} %get-tuple-element.12), channel_id=1, source_target_pairs={{1,0},{2,1},{3,2},{4,3},{5,4},{6,5},{7,6},{8,7},{9,8},{10,9},{11,1... | collective-permute-start | bytes 393224 | tf_op jit(solution)/shard_map/ppermute | solution.py:26
  7.0 15.0 %collective-permute-start = (bf16[1,16,1,4,1024]{4,1,3,2,0:T(8,128)(2,1)}, bf16[1,16,1,4,1024]{4,1,3,2,0:T(8,128)(2,1)S(1)}, u32[]{:S(2)}, u32[]{:S(2)}) collective-permute-start(bf16[1,16,1,4,1024]{4,1,3,2,0:T(8,128)(2,1)} %get-tuple-element.11), channel_id=1, source_target_pairs={{0,1},{1,2},{2,3},{3,4},{4,5},{5,6},{6,7},{7,8},{8,9},{9,10},{10,1... | collective-permute-start | bytes 393224 | tf_op jit(solution)/shard_map/ppermute | solution.py:23
  13.4 2.1 copy-start.23
  13.4 2.1 copy-start.22
  13.4 3.2 %copy-start.25 = (s32[2,16]{1,0:T(2,128)S(1)}, s32[2,16]{1,0:T(2,128)}, u32[]{:S(2)}) copy-start(s32[2,16]{1,0:T(2,128)} %param.19) | copy-start | bytes 388
  13.5 6.6 %copy-start.2 = (bf16[8,2560]{1,0:T(8,128)(2,1)S(1)}, bf16[8,2560]{1,0:T(8,128)(2,1)}, u32[]{:S(2)}) copy-start(bf16[8,2560]{1,0:T(8,128)(2,1)} %param.21) | copy-start | bytes 122884
  13.9 2.2 copy-start.26
  22.0 3.6 %copy-start.21 = (f32[1,1024]{1,0:T(1,128)S(1)}, f32[1,1024]{1,0:T(1,128)}, u32[]{:S(2)}) copy-start(f32[1,1024]{1,0:T(1,128)} %get-tuple-element.68) | copy-start | bytes 12292
  33.7 9.2 %collective-permute-start.3 = (bf16[1,16,1,4,1024]{4,1,3,2,0:T(8,128)(2,1)}, bf16[1,16,1,4,1024]{4,1,3,2,0:T(8,128)(2,1)S(1)}, u32[]{:S(2)}, u32[]{:S(2)}) collective-permute-start(bf16[1,16,1,4,1024]{4,1,3,2,0:T(8,128)(2,1)} %get-tuple-element.10), channel_id=1, source_target_pairs={{1,0},{2,1},{3,2},{4,3},{5,4},{6,5},{7,6},{8,7},{9,8},{10,9},{11,1... | collective-permute-start | bytes 393224 | tf_op jit(solution)/shard_map/ppermute | solution.py:26
  35.6 7.3 %collective-permute-start.2 = (bf16[1,16,1,4,1024]{4,1,3,2,0:T(8,128)(2,1)}, bf16[1,16,1,4,1024]{4,1,3,2,0:T(8,128)(2,1)S(1)}, u32[]{:S(2)}, u32[]{:S(2)}) collective-permute-start(bf16[1,16,1,4,1024]{4,1,3,2,0:T(8,128)(2,1)} %get-tuple-element.9), channel_id=1, source_target_pairs={{0,1},{1,2},{2,3},{3,4},{4,5},{5,6},{6,7},{7,8},{8,9},{9,10},{10,1... | collective-permute-start | bytes 393224 | tf_op jit(solution)/shard_map/ppermute | solution.py:23
  40.4 1.8 copy-start.24
  40.4 2.7 %copy-start.3 = (f32[1,1,1024]{2,0,1:T(1,128)S(1)}, f32[1,1,1024]{2,0,1:T(1,128)}, u32[]{:S(2)}) copy-start(f32[1,1,1024]{2,0,1:T(1,128)} %get-tuple-element.33) | copy-start | bytes 12292
  40.4 2.7 %copy-start.4 = (f32[1,1,1024]{2,0,1:T(1,128)S(1)}, f32[1,1,1024]{2,0,1:T(1,128)}, u32[]{:S(2)}) copy-start(f32[1,1,1024]{2,0,1:T(1,128)} %get-tuple-element.34) | copy-start | bytes 12292
  40.4 2.7 %copy-start.5 = (f32[1,1,1024]{2,0,1:T(1,128)S(1)}, f32[1,1,1024]{2,0,1:T(1,128)}, u32[]{:S(2)}) copy-start(f32[1,1,1024]{2,0,1:T(1,128)} %get-tuple-element.35) | copy-start | bytes 12292
  40.4 2.7 %copy-start.6 = (f32[1,1,1024]{2,0,1:T(1,128)S(1)}, f32[1,1,1024]{2,0,1:T(1,128)}, u32[]{:S(2)}) copy-start(f32[1,1,1024]{2,0,1:T(1,128)} %get-tuple-element.36) | copy-start | bytes 12292
  40.4 2.7 %copy-start.7 = (f32[1,1,1024]{2,0,1:T(1,128)S(1)}, f32[1,1,1024]{2,0,1:T(1,128)}, u32[]{:S(2)}) copy-start(f32[1,1,1024]{2,0,1:T(1,128)} %get-tuple-element.37) | copy-start | bytes 12292
  40.4 2.7 %copy-start.8 = (f32[1,1,1024]{2,0,1:T(1,128)S(1)}, f32[1,1,1024]{2,0,1:T(1,128)}, u32[]{:S(2)}) copy-start(f32[1,1,1024]{2,0,1:T(1,128)} %get-tuple-element.13) | copy-start | bytes 12292
  40.4 2.7 %copy-start.9 = (f32[1,1,1024]{2,0,1:T(1,128)S(1)}, f32[1,1,1024]{2,0,1:T(1,128)}, u32[]{:S(2)}) copy-start(f32[1,1,1024]{2,0,1:T(1,128)} %get-tuple-element.14) | copy-start | bytes 12292
  40.4 2.7 %copy-start.10 = (f32[1,1,1024]{2,0,1:T(1,128)S(1)}, f32[1,1,1024]{2,0,1:T(1,128)}, u32[]{:S(2)}) copy-start(f32[1,1,1024]{2,0,1:T(1,128)} %get-tuple-element.15) | copy-start | bytes 12292
  40.5 2.7 %copy-start.11 = (f32[1,1,1024]{2,0,1:T(1,128)S(1)}, f32[1,1,1024]{2,0,1:T(1,128)}, u32[]{:S(2)}) copy-start(f32[1,1,1024]{2,0,1:T(1,128)} %get-tuple-element.16) | copy-start | bytes 12292
  40.5 2.7 %copy-start.12 = (f32[1,1,1024]{2,0,1:T(1,128)S(1)}, f32[1,1,1024]{2,0,1:T(1,128)}, u32[]{:S(2)}) copy-start(f32[1,1,1024]{2,0,1:T(1,128)} %get-tuple-element.17) | copy-start | bytes 12292
  40.5 2.7 %copy-start.13 = (f32[1,1,1024]{2,0,1:T(1,128)S(1)}, f32[1,1,1024]{2,0,1:T(1,128)}, u32[]{:S(2)}) copy-start(f32[1,1,1024]{2,0,1:T(1,128)} %get-tuple-element.18) | copy-start | bytes 12292
  40.5 2.7 %copy-start.14 = (f32[1,1,1024]{2,0,1:T(1,128)S(1)}, f32[1,1,1024]{2,0,1:T(1,128)}, u32[]{:S(2)}) copy-start(f32[1,1,1024]{2,0,1:T(1,128)} %get-tuple-element.19) | copy-start | bytes 12292
  40.5 2.7 %copy-start.15 = (f32[1,1,1024]{2,0,1:T(1,128)S(1)}, f32[1,1,1024]{2,0,1:T(1,128)}, u32[]{:S(2)}) copy-start(f32[1,1,1024]{2,0,1:T(1,128)} %get-tuple-element.20) | copy-start | bytes 12292
  40.5 2.7 %copy-start.16 = (f32[1,1,1024]{2,0,1:T(1,128)S(1)}, f32[1,1,1024]{2,0,1:T(1,128)}, u32[]{:S(2)}) copy-start(f32[1,1,1024]{2,0,1:T(1,128)} %get-tuple-element.21) | copy-start | bytes 12292
  40.5 2.7 %copy-start.17 = (f32[1,1,1024]{2,0,1:T(1,128)S(1)}, f32[1,1,1024]{2,0,1:T(1,128)}, u32[]{:S(2)}) copy-start(f32[1,1,1024]{2,0,1:T(1,128)} %get-tuple-element.22) | copy-start | bytes 12292
  40.5 2.7 %copy-start.18 = (f32[1,1,1024]{2,0,1:T(1,128)S(1)}, f32[1,1,1024]{2,0,1:T(1,128)}, u32[]{:S(2)}) copy-start(f32[1,1,1024]{2,0,1:T(1,128)} %get-tuple-element.23) | copy-start | bytes 12292
  40.5 2.7 %copy-start.19 = (f32[1,1,1024]{2,0,1:T(1,128)S(1)}, f32[1,1,1024]{2,0,1:T(1,128)}, u32[]{:S(2)}) copy-start(f32[1,1,1024]{2,0,1:T(1,128)} %get-tuple-element.24) | copy-start | bytes 12292
  42.9 3.5 %copy-start.20 = (f32[1,1024]{1,0:T(1,128)S(1)}, f32[1,1024]{1,0:T(1,128)}, u32[]{:S(2)}) copy-start(f32[1,1024]{1,0:T(1,128)} %get-tuple-element.67) | copy-start | bytes 12292

commit v2 on v1

--- a/solution.py
+++ b/solution.py
@@ -15,48 +15,6 @@
 MESH = pl.DeviceIdType.MESH
 
 
-def extended(block, sides, width):
-    for axis, dim in sides:
-        count = lax.axis_size(axis)
-        forward = [(i, i + 1) for i in range(count - 1)]
-        backward = [(target, source) for source, target in forward]
-        low = lax.ppermute(
-            lax.slice_in_dim(block, block.shape[dim] - width, None, axis=dim), axis, forward
-        )
-        high = lax.ppermute(lax.slice_in_dim(block, 0, width, axis=dim), axis, backward)
-        block = jnp.concatenate([low, block, high], axis=dim)
-    return block
-
-
-def depth_block(padded, kernel, gains, weight):
-    frames = padded.shape[1]
-    height = padded.shape[2] - 2
-    breadth = padded.shape[3]
-    channels = padded.shape[4]
-    framed = jnp.pad(padded.astype(jnp.float32), ((0, 0), (2, 0), (0, 0), (1, 1), (0, 0)))
-    summed = jnp.zeros((padded.shape[0], frames, height, breadth, channels), jnp.float32)
-    for time_tap in range(3):
-        for row_tap in range(3):
-            for col_tap in range(3):
-                window = framed[
-                    :,
-                    time_tap : time_tap + frames,
-                    row_tap : row_tap + height,
-                    col_tap : col_tap + breadth,
-                    :,
-                ]
-                summed = summed + window * kernel[9 * time_tap + 3 * row_tap + col_tap].astype(
-                    jnp.float32
-                )
-    factor = lax.rsqrt(jnp.mean(summed * summed, axis=-1, keepdims=True) + 1e-05)
-    normed = (summed * factor * gains.astype(jnp.float32)).astype(jnp.bfloat16)
-    projected = jnp.dot(
-        normed.reshape(-1, channels), weight, preferred_element_type=jnp.float32
-    ).reshape(summed.shape)
-    centre = padded[:, :, 1:-1].astype(jnp.float32)
-    return (centre + jax.nn.gelu(projected)).astype(jnp.bfloat16)
-
-
 def gelu(z):
     return 0.5 * z * (1.0 + jnp.tanh(0.7978845608028654 * (z + 0.044715 * (z * z * z))))
 
@@ -73,7 +31,10 @@
     pack_ref,
     in_ref,
     aux_ref,
-    latent_ref,
+    start_ref,
+    taps_ref,
+    gains_ref,
+    point_ref,
     pick_ref,
     out_ref,
     w_all,
@@ -83,6 +44,12 @@
     embeds,
     squares,
     mixed,
+    halos,
+    middle,
+    conv,
+    latent_ref,
+    h_send,
+    h_recv,
     w_send,
     w_recv,
     i_send,
@@ -121,6 +88,9 @@
         return ((d + shift) % D, seq)
 
     peers = [to_c(s) for s in range(1, C)] + [to_t(b) for b in bits] + [to_d(s) for s in range(1, D)]
+    S = C * T
+    above, below = (d, (seq + S - 1) % S), (d, (seq + 1) % S)
+    peers += [above, below]
     barrier = pltpu.get_barrier_semaphore()
     for peer in peers:
         pl.semaphore_signal(barrier, inc=1, device_id=peer, device_id_type=MESH)
@@ -194,19 +164,22 @@
     own = [
         pltpu.make_async_copy(pack_ref.at[c], w_slot(0, 0), own_sem.at[0]),
         pltpu.make_async_copy(in_ref, i_slot(0, 0, 0), own_sem.at[1]),
-        pltpu.make_async_copy(latent_ref, l_slot(0, 0), own_sem.at[2]),
         pltpu.make_async_copy(aux_ref, a_slot(0), own_sem.at[3]),
     ]
     for copy in own:
         copy.start()
+    height, breadth, frames, channels = start_ref.shape
+
+    def share_rows(l, source):
+        push(source.at[height - 1], halos.at[l, 0], h_send.at[l, 0], h_recv.at[l, 0], below)
+        push(source.at[0], halos.at[l, 1], h_send.at[l, 1], h_recv.at[l, 1], above)
+
+    share_rows(0, start_ref)
     for shift in range(1, D):
         push(aux_ref, a_slot(0), a_send.at[shift], a_recv.at[shift], to_d(shift))
     for shift in range(1, C):
         push(in_ref, i_slot(0, 0, 0), i_send.at[shift, 0, 0], i_recv.at[shift, 0, 0], to_c(shift))
     i_forward(0, 0, 0, in_ref)
-    for shift in range(1, C):
-        push(latent_ref, l_slot(0, 0), l_send.at[shift, 0], l_recv.at[shift, 0], to_c(shift))
-    l_forward(0, latent_ref)
     for shift in range(1, C):
         push(
             pack_ref.at[(c + shift) % C],
@@ -231,13 +204,81 @@
         if e == 0:
             l_forward(s, l_slot(s, e))
 
+    lanes = 256
+
+    def encode(l, source):
+        arrived(halos.at[l, 0], h_recv.at[l, 0])
+        arrived(halos.at[l, 1], h_recv.at[l, 1])
+        frame_ids = lax.broadcasted_iota(jnp.int32, (frames, lanes), 0)
+
+        def lane_step(j, carry):
+            cols = pl.ds(pl.multiple_of(j * lanes, lanes), lanes)
+            taps = taps_ref[l, :, cols].astype(jnp.float32)
+
+            def patch(r, w):
+                if r < 0:
+                    return jnp.where(seq > 0, halos[l, 0, w, :, cols].astype(jnp.float32), 0.0)
+                if r == height:
+                    return jnp.where(seq < S - 1, halos[l, 1, w, :, cols].astype(jnp.float32), 0.0)
+                return source[r, w, :, cols].astype(jnp.float32)
+
+            for r in range(height):
+                for w in range(breadth):
+                    sums = [None] * 3
+                    for b in range(3):
+                        for k in range(3):
+                            if not 0 <= w + k - 1 < breadth:
+                                continue
+                            value = patch(r + b - 1, w + k - 1)
+                            for a in range(3):
+                                tap = 9 * a + 3 * b + k
+                                term = value * taps[tap : tap + 1]
+                                sums[a] = term if sums[a] is None else sums[a] + term
+                    total = sums[2]
+                    for a in range(2):
+                        moved = pltpu.roll(sums[a], 2 - a, 0)
+                        total = total + jnp.where(frame_ids >= 2 - a, moved, 0.0)
+                    base = (r * breadth + w) * frames
+                    conv[base : base + frames, cols] = total
+            return carry
+
+        lax.fori_loop(0, channels // lanes, lane_step, 0)
+        summed = conv[...]
+        factor = lax.rsqrt(jnp.mean(summed * summed, axis=-1, keepdims=True) + 1e-05)
+        gain = gains_ref[l].astype(jnp.float32)
+        normed = (summed * factor * gain[None]).astype(jnp.bfloat16)
+        projected = jnp.dot(normed, point_ref[l], preferred_element_type=jnp.float32)
+        change = gelu(projected)
+        for r in range(height):
+            for w in range(breadth):
+                base = (r * breadth + w) * frames
+                value = source[r, w].astype(jnp.float32) + change[base : base + frames]
+                value = value.astype(jnp.bfloat16)
+                if l + 1 < point_ref.shape[0]:
+                    middle[l, r, w] = value
+                else:
+                    latent_ref[base : base + frames] = value
+
+    source = start_ref
+    for l in range(point_ref.shape[0]):
+        encode(l, source)
+        if l + 1 < point_ref.shape[0]:
+            source = middle.at[l]
+            share_rows(l + 1, source)
+            for s in range(1, C):
+                i_event(s, 0, 0)
+    for shift in range(1, C):
+        push(latent_ref, l_slot(0, 0), l_send.at[shift, 0], l_recv.at[shift, 0], to_c(shift))
+    l_forward(0, latent_ref)
+    latent_copy = pltpu.make_async_copy(latent_ref, l_slot(0, 0), own_sem.at[2])
+    latent_copy.start()
+    own.append(latent_copy)
+
     order_w = sorted(
         ((m.bit_count(), s, m) for s in range(C) for m in range(T) if s or m),
         key=lambda item: (item[0] + item[1], item[0]),
     )
     w_todo = [(s, m) for _, s, m in order_w]
-    for s in range(1, C):
-        i_event(s, 0, 0)
     for m in sorted((m for m in range(1, T) if not m & last), key=lambda m: m.bit_count()):
         for s in range(C):
             i_event(s, m, 0)
@@ -295,7 +336,7 @@
 
     row_ids = lax.broadcasted_iota(jnp.int32, (tokens, tokens), 0)
     col_ids = lax.broadcasted_iota(jnp.int32, (tokens, tokens), 1)
-    seen = (row_ids % cells == col_ids % cells) & (row_ids // cells >= col_ids // cells)
+    seen = (row_ids // frames == col_ids // frames) & (row_ids >= col_ids)
 
     def unit(x):
         return x * lax.rsqrt(jnp.mean(x * x, axis=-1, keepdims=True) + 1e-06)
@@ -385,6 +426,7 @@
     kvg = kv_local // C
     group = Q_HEADS // KV_HEADS
     depth = w_query.shape[0]
+    frames_first = (0, 3, 1, 2, 4)
 
     flat_index = patch_index.reshape(-1)
     position_pick = (flat_index[:, None] == jnp.arange(positions, dtype=jnp.int32)[None, :]).astype(
@@ -394,12 +436,7 @@
         tiles.shape
     )
     hidden = (tiles.astype(jnp.float32) + placed).astype(jnp.bfloat16)
-    for block_idx in range(blocks):
-        padded = extended(hidden, (("seq", 2),), 1)
-        hidden = depth_block(
-            padded, depth_kernel[block_idx], enc_gain[block_idx], point_weight[block_idx]
-        )
-    latent = jnp.take(hidden, seq_order, axis=3).reshape(-1, channels)
+    start = hidden[0].transpose(1, 2, 0, 3)
 
     cells = height * breadth
     tokens = frames * cells
@@ -416,7 +453,7 @@
         [action_table, dyn_gain[None], jnp.zeros((7, action_table.shape[1]), jnp.bfloat16)], axis=0
     )
     pick = (
-        jnp.repeat(action_ids.reshape(-1), cells)[:, None] == jnp.arange(16, dtype=jnp.int32)[None]
+        jnp.tile(action_ids[:, None, :], (1, cells, 1)).reshape(-1)[:, None] == jnp.arange(16, dtype=jnp.int32)[None]
     ).astype(jnp.bfloat16)
     width = pack.shape[2]
     qcols = kvg * group * HEAD
@@ -425,7 +462,7 @@
     out = pl.pallas_call(
         functools.partial(window_kernel, (D, C, T, cells, kvg)),
         out_shape=jax.ShapeDtypeStruct((D * tokens, C * qcols), bf16),
-        in_specs=[pl.BlockSpec(memory_space=pltpu.VMEM)] * 5,
+        in_specs=[pl.BlockSpec(memory_space=pltpu.VMEM)] * 8,
         out_specs=pl.BlockSpec(memory_space=pltpu.VMEM),
         scratch_shapes=[
             pltpu.VMEM((S * depth, width), bf16),
@@ -435,6 +472,12 @@
             pltpu.VMEM((C, D * tokens, DIM), bf16),
             pltpu.VMEM((C, D * tokens, HEAD), f32),
             pltpu.VMEM((C, D * tokens, qcols), bf16),
+            pltpu.VMEM((blocks, 2, breadth, frames, channels), bf16),
+            pltpu.VMEM((max(blocks - 1, 1), height, breadth, frames, channels), bf16),
+            pltpu.VMEM((tokens, channels), f32),
+            pltpu.VMEM((tokens, channels), bf16),
+            dma((blocks, 2)),
+            dma((blocks, 2)),
             dma((C, T)),
             dma((C, T)),
             dma((C, T, D)),
@@ -450,8 +493,9 @@
         compiler_params=pltpu.CompilerParams(
             collective_id=0, has_side_effects=True, vmem_limit_bytes=60 * 1024 * 1024
         ),
-    )(pack, w_in, aux, latent, pick)
-    return out.reshape(D, frames, height, breadth, -1)
+    )(pack, w_in, aux, start, depth_kernel, enc_gain, point_weight, pick)
+    out = out.reshape(D, height, breadth, frames, -1).transpose(frames_first)
+    return jnp.take(out, seq_order, axis=3)
 
 
 def solution(mesh):

time: 232 us -> 210 us (0.905)
  the two profiles are of different devices: /device:TPU:7 before, /device:TPU:9 now
where the time goes in v2:
time: 210 us
  Pallas kernels  194 us (92%)
  local copies, waits for them, and re-layouts  10.7 us (5%)
  other arithmetic  4.38 us (2%)
    pallas_call x1, Pallas kernels, body(): pl.pallas_call(functools.partial(window_kernel, (D, C, T, cells, kvg)), o...  194 us

profile of v2, /device:TPU:9, one launch (start us, length us, event | category | flops | bytes accessed | tf_op | source)
XLA Modules:
  0.0 210.0 jit_solution(16619851046340161356)
XLA Ops:
  0.0 0.0 copy-start
  0.0 1.6 copy.35
  1.6 0.0 copy-done
  1.7 1.3 bitcast_bitcast_fusion.1
  2.9 2.2 %reshape.29 = bf16[4,320,256]{2,1,0:T(8,128)(2,1)S(1)} reshape(bf16[4,320,2,128]{3,2,1,0:T(2,128)(2,1)} %bitcast_bitcast_fusion.1) | data formatting | bytes 1310720 | tf_op jit(solution)/shard_map/reshape | solution.py:446
  5.2 0.0 copy-start.6
  5.2 0.0 copy-start.1
  5.2 1.6 pad_maximum_fusion.pack_ref
  6.8 0.0 copy-done.6
  6.8 0.0 copy-start.4
  6.8 0.1 copy.21
  6.9 0.1 eq.28
  7.0 0.0 copy-done.1
  7.1 0.0 copy-start.7
  7.1 0.3 fusion.3
  7.3 0.1 reshape.30
  7.5 0.3 copy-done.2
  7.8 1.1 fusion.1.start_ref
  8.9 0.0 copy-done.3
  8.9 0.7 copy.23.taps_ref
  9.6 0.0 copy-done.5
  9.6 0.1 pad.2.clone
  9.7 0.0 copy-done.4
  9.7 0.7 maximum_maximum_fusion.aux_ref
  10.4 0.0 copy-done.7
  10.4 0.1 tile.8
  10.5 0.7 fusion.2.pick_ref
  11.2 194.5 %shard_map.127 = bf16[256,2560]{1,0:T(8,128)(2,1)} custom-call(bf16[4,320,896]{2,1,0:T(8,128)(2,1)} %pad_maximum_fusion.pack_ref, bf16[64,2560]{1,0:T(8,128)(2,1)} %in_ref.1, bf16[16,2560]{1,0:T(8,128)(2,1)} %maximum_maximum_fusion.aux_ref, bf16[2,4,16,1024]{3,2,1,0:T(8,128)(2,1)} %fusion.1.start_ref, bf16[2,27,1024]{2,1,0:T(8,128)(2,1)} %copy.23.taps_ref, ...), custom_call_target="tpu_custom_call" | custom-call | tf_op jit(solution)/shard_map/pallas_call | solution.py:462
  205.7 0.0 copy-done.8
  205.7 1.9 gather_fusion
  207.7 0.2 select_bitcast_fusion
  207.9 2.1 copy.24
  (10 shorter events, 0.1 us)
Async XLA Ops:
  0.0 1.6 copy-start
  5.2 1.6 copy-start.6
  5.2 1.9 copy-start.1
  6.8 1.0 copy-start.2
  6.8 2.1 copy-start.3
  6.8 2.8 %copy-start.5 = (bf16[2560]{0:T(1024)(128)(2,1)S(1)}, bf16[2560]{0:T(1024)(128)(2,1)}, u32[]{:S(2)}) copy-start(bf16[2560]{0:T(1024)(128)(2,1)} %param.22) | copy-start | bytes 15364
  6.8 2.9 %copy-start.4 = (bf16[8,2560]{1,0:T(8,128)(2,1)S(1)}, bf16[8,2560]{1,0:T(8,128)(2,1)}, u32[]{:S(2)}) copy-start(bf16[8,2560]{1,0:T(8,128)(2,1)} %param.21) | copy-start | bytes 122884
  7.1 3.3 %copy-start.7 = (s32[2,16]{1,0:T(2,128)S(1)}, s32[2,16]{1,0:T(2,128)}, u32[]{:S(2)}) copy-start(s32[2,16]{1,0:T(2,128)} %param.19) | copy-start | bytes 388
  11.2 194.5 %copy-start.8 = (s32[4]{0:T(128)S(1)}, s32[4]{0:T(128)}, u32[]{:S(2)}) copy-start(s32[4]{0:T(128)} %param.25) | copy-start | bytes 52
